TPU v7x, 32 devices: a whole 2x2x4 slice. The times are simulated.
32 devices in a mesh: groups: 2 (over x), freq: 8 (over z, y), gvec: 2 (over core).
Axes of the slice: x: 2, y: 2, z: 4, core: 2. Of those that a mesh axis runs over, the one named last changes fastest.
Arguments:
- screened: bfloat16 [16, 3072, 3072], P(('groups', 'freq'), 'gvec'), parts along dimension 0, may hold values from -0.109375 to 0.109375
- densities: bfloat16 [6144, 512], P(('groups', 'gvec'), 'freq'), parts along dimension 0, may hold values from -0.8046875 to 0.8046875
- pair_order: int32 [512], replicated, may hold values from 0 to 511, each once
- quad_index: int32 [4, 8], replicated, may hold values from 0 to 63
- quad_table: float32 [64], replicated, may hold values from 0.05 to 0.5
Outputs:
- kernel_out: float32 [8, 512, 512], P('groups', 'freq', 'gvec'), parts along dimension 0
There are 2 independent parts, one for each index of `groups`. A program takes and returns all parts, laid end to end along the dimension named above; an argument that names none is the same for every part. Nothing has to cross between parts.
All inputs are finite; a program needn't handle non-finite values.
Results may differ from a plain program's by a relative error of at most 0.0029.
Values may be sent and summed in bfloat16 or wider, within the bound.
No kernel may reach another device: no remote copies, remote signals or barrier semaphores. Data moves between devices by JAX's collectives and lax.ppermute only.
A program may use at most 64 MiB of HBM per device.

v0:
```python
import jax
import jax.numpy as jnp
from jax import lax
from jax.sharding import PartitionSpec as P


def body(screened, densities, pair_order, quad_index, quad_table):
    screen = screened[0]
    own_rows = lax.all_gather(densities, "freq", axis=1, tiled=True)
    own_rows = jnp.take(own_rows, pair_order, axis=1)
    product = jnp.dot(
        screen,
        lax.all_gather(own_rows, "gvec", axis=0, tiled=True),
        preferred_element_type=jnp.float32,
    )
    product = product.astype(jnp.bfloat16)
    kernel = lax.dot_general(
        own_rows, product, (((0,), (0,)), ((), ())), preferred_element_type=jnp.float32
    )
    table_size = quad_table.shape[0]
    onehot = (
        quad_index[:, :, None] == jnp.arange(table_size, dtype=jnp.int32)[None, None, :]
    ).astype(jnp.float32)
    weights = jnp.sum(onehot * quad_table[None, None, :], axis=2)
    halves = lax.psum_scatter(kernel, "gvec", scatter_dimension=1, tiled=True)
    return jnp.einsum(
        "of,fij->oij",
        weights,
        lax.all_to_all(halves[None], "freq", split_axis=1, concat_axis=0, tiled=True),
        precision=lax.Precision.HIGHEST,
    )


def solution(mesh):
    placed = (P(("groups", "freq"), "gvec", None), P(("groups", "gvec"), "freq"), P(), P(), P())
    return jax.shard_map(
        body, mesh=mesh, in_specs=placed, out_specs=P("groups", "freq", "gvec"), check_vma=False
    )
```

profile of v0, /device:TPU:0, one launch (start us, length us, event | category | flops | bytes accessed | tf_op | source)
XLA Modules:
  0.0 126.2 jit_solution(10194464482765181643)
XLA Ops:
  6.5 0.0 all-gather.3.cloned.1.call-start
  6.5 0.7 all-gather.3.cloned.1.call-update
  7.3 0.0 all-gather.5.cloned.1.call-start
  7.3 0.7 compare_select_fusion
  8.0 0.7 compare_and_fusion
  8.7 47.8 %all-gather.3.cloned.1.call-done = bf16[1536,512]{0,1:T(8,128)(2,1)} async-done(((bf16[1536,64]{0,1:T(8,128)(2,1)}), bf16[1536,512]{0,1:T(8,128)(2,1)}) %all-gather.3.cloned.1.call-update) | async-done | bytes 1572880 | tf_op jit(solution)/shard_map/all_gather | solution.py:9
  56.5 5.2 %gather_fusion = bf16[512,1536]{1,0:T(8,128)(2,1)S(1)} fusion(bf16[1536,512]{0,1:T(8,128)(2,1)} %all-gather.3.cloned.1.call-done, s32[1024]{0:T(1024)S(1)} %pad_clamp_fusion), kind=kCustom, calls=%fused_computation | custom fusion | bytes 3147776 | tf_op jit(solution)/shard_map/jit(_take)/gather | solution.py:10
  61.7 1.4 %fusion.6 = bf16[1536,512]{0,1:T(8,128)(2,1)} fusion(bf16[512,1536]{1,0:T(8,128)(2,1)S(1)} %gather_fusion, pred[512]{0:T(512)(128)(4,1)S(1)} %compare_and_fusion), kind=kLoop, calls=%fused_computation.6 | loop fusion | flops 786432 | bytes 3146240 | tf_op jit(solution)/shard_map/jit(_take)/select_n | solution.py:10
  63.0 0.0 all-gather.5.cloned.1.call-update
  63.1 0.0 reduce-scatter.2.cloned.1.call-start
  63.1 10.6 %all-gather.5.cloned.1.call-done = bf16[3072,512]{0,1:T(8,128)(2,1)} async-done(((bf16[1536,512]{0,1:T(8,128)(2,1)}), bf16[3072,512]{0,1:T(8,128)(2,1)}) %all-gather.5.cloned.1.call-update) | async-done | bytes 3145744 | tf_op jit(solution)/shard_map/all_gather | solution.py:13
  73.7 11.5 %fusion.5 = f32[512,512]{1,0:T(8,128)} fusion(bf16[512,1536]{1,0:T(8,128)(2,1)S(1)} %gather_fusion, pred[512]{0:T(512)(128)(4,1)S(1)} %compare_and_fusion, bf16[3072,512]{0,1:T(8,128)(2,1)} %all-gather.5.cloned.1.call-done, bf16[1,1536,3072]{2,1,0:T(8,128)(2,1)} %param.5), kind=kOutput, calls=%fused_computation.5 | convolution fusion | flops 5638717440 | bytes 15204864 | tf_op jit(solution)/shard_map/dot_general | solution.py:17
  85.2 0.0 copy-start
  85.2 0.0 copy-start.1
  85.2 0.0 reduce-scatter.2.cloned.1.call-update
  85.2 9.7 %reduce-scatter.2.cloned.1.call-done = f32[512,256]{1,0:T(8,128)} async-done(((f32[512,512]{1,0:T(8,128)}), f32[512,256]{1,0:T(8,128)}) %reduce-scatter.2.cloned.1.call-update) | async-done | bytes 524304 | tf_op jit(solution)/shard_map/reduce_scatter | solution.py:25
  95.0 2.4 %copy.13 = f32[1,512,256]{2,0,1:T(1,128)} copy(f32[1,512,256]{2,1,0:T(8,128)} %bitcast.16) | data formatting | bytes 1048576 | tf_op jit(solution)/shard_map/broadcast_in_dim | solution.py:29
  97.3 5.8 %all-to-all-start = ((f32[1,512,256]{2,0,1:T(1,128)}), f32[1,512,256]{2,0,1:T(1,128)S(1)}, u32[]{:S(2)}, u32[]{:S(2)}) async-start(f32[1,512,256]{2,0,1:T(1,128)} %copy.13), calls=%async_computation.1 | async-start | bytes 1048576 | tf_op jit(solution)/shard_map/all_to_all | solution.py:29
  103.1 0.0 copy-done
  103.1 0.0 copy-done.1
  103.1 0.2 select_reduce_fusion
  103.3 14.8 %all-to-all-done = f32[1,512,256]{2,0,1:T(1,128)S(1)} async-done(((f32[1,512,256]{2,0,1:T(1,128)}), f32[1,512,256]{2,0,1:T(1,128)S(1)}, u32[]{:S(2)}, u32[]{:S(2)}) %all-to-all-start) | async-done | bytes 524320 | tf_op jit(solution)/shard_map/all_to_all | solution.py:29
  118.1 0.8 fusion.9
  118.9 0.8 copy.15
  (2 shorter events, 0.0 us)
Async XLA Ops:
  6.5 49.9 %all-gather.3.cloned.1.call-start = ((), (), s32[]{:S(2)}) async-start(), calls=%async_computation.2 | async-start | bytes 1769472 | tf_op jit(solution)/shard_map/all_gather | solution.py:9
  7.3 66.4 %all-gather.5.cloned.1.call-start = ((), (), s32[]{:S(2)}) async-start(), calls=%async_computation.3 | async-start | bytes 4718592 | tf_op jit(solution)/shard_map/all_gather | solution.py:13
  63.1 31.9 %reduce-scatter.2.cloned.1.call-start = ((), (), s32[]{:S(2)}) async-start(), calls=%async_computation.4 | async-start | bytes 1572864 | tf_op jit(solution)/shard_map/reduce_scatter | solution.py:25
  85.2 17.9 %copy-start = (s32[4,8]{1,0:T(4,128)S(1)}, s32[4,8]{1,0:T(4,128)}, u32[]{:S(2)}) copy-start(s32[4,8]{1,0:T(4,128)} %param.8) | copy-start | bytes 388
  85.2 17.9 %copy-start.1 = (f32[64]{0:T(128)S(1)}, f32[64]{0:T(128)}, u32[]{:S(2)}) copy-start(f32[64]{0:T(128)} %param.9) | copy-start | bytes 772
  97.3 20.7 %all-to-all-start = ((f32[1,512,256]{2,0,1:T(1,128)}), f32[1,512,256]{2,0,1:T(1,128)S(1)}, u32[]{:S(2)}, u32[]{:S(2)}) async-start(f32[1,512,256]{2,0,1:T(1,128)} %copy.13), calls=%async_computation.1 | async-start | bytes 1048576 | tf_op jit(solution)/shard_map/all_to_all | solution.py:29
Sparse Core Ops, SparseCore 0:
  9.5 46.8 all-gather.2
  63.2 10.4 all-gather.4
  85.3 9.5 reduce-scatter.1
where the time goes:
time: 126 us
  waiting for transfers between devices  83.6 us (66%)
  between operations  13.1 us (10%)
  matrix products  12.3 us (10%)
  local copies, waits for them, and re-layouts  8.37 us (7%)
  starting transfers between devices  5.84 us (5%)
  other arithmetic  2.9 us (2%)
    all_gather x1, waiting for transfers between devices, body(): own_rows = lax.all_gather(densities, 'freq', axis=1, tiled=True)  47.8 us
    all_to_all x1, waiting for transfers between devices, body(): lax.all_to_all(halves[None], 'freq', split_axis=1, concat_axis=0, tiled=T...  14.8 us
    dot_general x1, matrix products, body(): lax.dot_general(own_rows, product, (((0,), (0,)), ((), ())), preferred_el...  11.5 us
    all_gather x1, waiting for transfers between devices, body(): lax.all_gather(own_rows, 'gvec', axis=0, tiled=True)  10.6 us
    reduce_scatter x1, waiting for transfers between devices, body(): halves = lax.psum_scatter(kernel, 'gvec', scatter_dimension=1, tiled=True)  9.73 us
    all_to_all x1, starting transfers between devices, body(): lax.all_to_all(halves[None], 'freq', split_axis=1, concat_axis=0, tiled=T...  5.76 us
    gather x1, local copies, waits for them, and re-layouts, body(): own_rows = jnp.take(own_rows, pair_order, axis=1)  5.21 us
  transfers between devices with their start and end apart: 4, of which 4 were waited for; matrix products, arithmetic and copies ran while one was open for 1% of the time, Pallas kernels for 0%

commit v1 on v0

--- a/solution.py
+++ b/solution.py
@@ -6,7 +6,25 @@
 
 def body(screened, densities, pair_order, quad_index, quad_table):
     screen = screened[0]
-    own_rows = lax.all_gather(densities, "freq", axis=1, tiled=True)
+    length, here, rows = (lax.axis_size("freq"), lax.axis_index("freq"), densities.shape[1])
+    right = [(i, (i + 1) % length) for i in range(length)]
+    backward = [(i, (i - 1) % length) for i in range(length)]
+    own_rows = jnp.zeros(
+        (*densities.shape[:1], length * rows, *densities.shape[1 + 1 :]), densities.dtype
+    )
+    own_rows = lax.dynamic_update_slice_in_dim(own_rows, densities, here * rows, axis=1)
+    from_left = from_right = densities
+    halfway = length // 2
+    for step in range(1, halfway + 1):
+        from_left = lax.ppermute(from_left, "freq", right)
+        own_rows = lax.dynamic_update_slice_in_dim(
+            own_rows, from_left, (here - step) % length * rows, axis=1
+        )
+        if step < length - halfway:
+            from_right = lax.ppermute(from_right, "freq", backward)
+            own_rows = lax.dynamic_update_slice_in_dim(
+                own_rows, from_right, (here + step) % length * rows, axis=1
+            )
     own_rows = jnp.take(own_rows, pair_order, axis=1)
     product = jnp.dot(
         screen,

time: 126 us -> 116 us (0.921)
  waiting for transfers between devices: 83.6 us -> 57.1 us
  starting transfers between devices: 5.84 us -> 25.4 us
  local copies, waits for them, and re-layouts: 8.37 us -> 5.57 us
    all_gather x1 -> x0, waiting for transfers between devices: 47.8 us -> none  [body(): own_rows = lax.all_gather(densities, 'freq', axis=1, tiled=True)]
    ppermute x0 -> x7, waiting for transfers between devices: none -> 21.6 us  [the longest x4 21.6 us: body(): from_left = lax.ppermute(from_left, 'freq', right)]
    ppermute x0 -> x7, starting transfers between devices: none -> 19.6 us  [the longest x3 10.5 us: body(): from_right = lax.ppermute(from_right, 'freq', backward)]
    gather x1, local copies, waits for them, and re-layouts: 5.21 us -> 2.14 us  [body(): own_rows = jnp.take(own_rows, pair_order, axis=1)]
  transfers between devices with their start and end apart: 4 -> 10, of which waited for: 4 -> 7; matrix products, arithmetic and copies ran while one was open for 1% -> 1% of each run, Pallas kernels for 0% -> 0%
where the time goes in v1:
time: 116 us
  waiting for transfers between devices  57.1 us (49%)
  starting transfers between devices  25.4 us (22%)
  between operations  13.6 us (12%)
  matrix products  12.3 us (11%)
  local copies, waits for them, and re-layouts  5.57 us (5%)
  other arithmetic  2.23 us (2%)
    ppermute x4, waiting for transfers between devices, body(): from_left = lax.ppermute(from_left, 'freq', right)  21.6 us
    all_to_all x1, waiting for transfers between devices, body(): lax.all_to_all(halves[None], 'freq', split_axis=1, concat_axis=0, tiled=T...  14.8 us
    dot_general x1, matrix products, body(): lax.dot_general(own_rows, product, (((0,), (0,)), ((), ())), preferred_el...  11.5 us
    all_gather x1, waiting for transfers between devices, body(): lax.all_gather(own_rows, 'gvec', axis=0, tiled=True)  10.9 us
    ppermute x3, starting transfers between devices, body(): from_right = lax.ppermute(from_right, 'freq', backward)  10.5 us
    reduce_scatter x1, waiting for transfers between devices, body(): halves = lax.psum_scatter(kernel, 'gvec', scatter_dimension=1, tiled=True)  9.7 us
    ppermute x4, starting transfers between devices, body(): from_left = lax.ppermute(from_left, 'freq', right)  9.03 us
    all_to_all x1, starting transfers between devices, body(): lax.all_to_all(halves[None], 'freq', split_axis=1, concat_axis=0, tiled=T...  5.78 us
  transfers between devices with their start and end apart: 10, of which 7 were waited for; matrix products, arithmetic and copies ran while one was open for 1% of the time, Pallas kernels for 0%

profile of v1, /device:TPU:0, one launch (start us, length us, event | category | flops | bytes accessed | tf_op | source)
XLA Modules:
  0.0 116.1 jit_solution(4316216843737223518)
XLA Ops:
  6.5 0.0 copy-start
  6.5 0.0 copy-start.1
  6.5 0.0 all-gather.2.cloned.1.call-start
  6.5 3.0 %collective-permute-start = (bf16[1536,64]{0,1:T(8,128)(2,1)}, bf16[1536,64]{0,1:T(8,128)(2,1)S(1)}, u32[]{:S(2)}, u32[]{:S(2)}) collective-permute-start(bf16[1536,64]{0,1:T(8,128)(2,1)} %param.6), channel_id=1, source_target_pairs={{0,2},{2,4},{4,6},{6,8},{8,10},{10,12},{12,14},{14,0},{1,3},{3,5},... | collective-permute-start | bytes 589832 | tf_op jit(solution)/shard_map/ppermute | solution.py:19
  9.5 3.1 %collective-permute-start.1 = (bf16[1536,64]{0,1:T(8,128)(2,1)}, bf16[1536,64]{0,1:T(8,128)(2,1)S(1)}, u32[]{:S(2)}, u32[]{:S(2)}) collective-permute-start(bf16[1536,64]{0,1:T(8,128)(2,1)} %param.6), channel_id=1, source_target_pairs={{0,14},{2,0},{4,2},{6,4},{8,6},{10,8},{12,10},{14,12},{1,15},{3,1}... | collective-permute-start | bytes 589832 | tf_op jit(solution)/shard_map/ppermute | solution.py:24
  12.6 0.7 compare_select_fusion
  13.3 0.1 broadcast_in_dim.22
  13.4 0.0 copy-done
  13.5 0.0 copy-done.1
  13.5 4.7 %collective-permute-done = bf16[1536,64]{0,1:T(8,128)(2,1)S(1)} collective-permute-done((bf16[1536,64]{0,1:T(8,128)(2,1)}, bf16[1536,64]{0,1:T(8,128)(2,1)S(1)}, u32[]{:S(2)}, u32[]{:S(2)}) %collective-permute-start) | collective-permute-done | bytes 196640 | tf_op jit(solution)/shard_map/ppermute | solution.py:19
  18.2 2.4 %collective-permute-start.2 = (bf16[1536,64]{0,1:T(8,128)(2,1)S(1)}, bf16[1536,64]{0,1:T(8,128)(2,1)S(1)}, u32[]{:S(2)}, u32[]{:S(2)}) collective-permute-start(bf16[1536,64]{0,1:T(8,128)(2,1)S(1)} %collective-permute-done), channel_id=1, source_target_pairs={{0,2},{2,4},{4,6},{6,8},{8,10},{10,12},{12,14},{14,0},{1,3},{3,5},... | collective-permute-start | bytes 589832 | tf_op jit(solution)/shard_map/ppermute | solution.py:19
  20.6 0.0 collective-permute-done.1
  20.6 3.0 %collective-permute-start.3 = (bf16[1536,64]{0,1:T(8,128)(2,1)S(1)}, bf16[1536,64]{0,1:T(8,128)(2,1)S(1)}, u32[]{:S(2)}, u32[]{:S(2)}) collective-permute-start(bf16[1536,64]{0,1:T(8,128)(2,1)S(1)} %collective-permute-done.1), channel_id=1, source_target_pairs={{0,14},{2,0},{4,2},{6,4},{8,6},{10,8},{12,10},{14,12},{1,15},{3,1}... | collective-permute-start | bytes 589832 | tf_op jit(solution)/shard_map/ppermute | solution.py:24
  23.7 4.4 %collective-permute-done.2 = bf16[1536,64]{0,1:T(8,128)(2,1)S(1)} collective-permute-done((bf16[1536,64]{0,1:T(8,128)(2,1)S(1)}, bf16[1536,64]{0,1:T(8,128)(2,1)S(1)}, u32[]{:S(2)}, u32[]{:S(2)}) %collective-permute-start.2) | collective-permute-done | bytes 196640 | tf_op jit(solution)/shard_map/ppermute | solution.py:19
  28.1 2.5 %collective-permute-start.4 = (bf16[1536,64]{0,1:T(8,128)(2,1)S(1)}, bf16[1536,64]{0,1:T(8,128)(2,1)S(1)}, u32[]{:S(2)}, u32[]{:S(2)}) collective-permute-start(bf16[1536,64]{0,1:T(8,128)(2,1)S(1)} %collective-permute-done.2), channel_id=1, source_target_pairs={{0,2},{2,4},{4,6},{6,8},{8,10},{10,12},{12,14},{14,0},{1,3},{3,5},... | collective-permute-start | bytes 589832 | tf_op jit(solution)/shard_map/ppermute | solution.py:19
  30.6 0.0 collective-permute-done.3
  30.6 4.4 %collective-permute-start.5 = (bf16[1536,64]{0,1:T(8,128)(2,1)S(1)}, bf16[1536,64]{0,1:T(8,128)(2,1)S(1)}, u32[]{:S(2)}, u32[]{:S(2)}) collective-permute-start(bf16[1536,64]{0,1:T(8,128)(2,1)S(1)} %collective-permute-done.3), channel_id=1, source_target_pairs={{0,14},{2,0},{4,2},{6,4},{8,6},{10,8},{12,10},{14,12},{1,15},{3,1}... | collective-permute-start | bytes 589832 | tf_op jit(solution)/shard_map/ppermute | solution.py:24
  35.0 3.7 %collective-permute-done.4 = bf16[1536,64]{0,1:T(8,128)(2,1)S(1)} collective-permute-done((bf16[1536,64]{0,1:T(8,128)(2,1)S(1)}, bf16[1536,64]{0,1:T(8,128)(2,1)S(1)}, u32[]{:S(2)}, u32[]{:S(2)}) %collective-permute-start.4) | collective-permute-done | bytes 196640 | tf_op jit(solution)/shard_map/ppermute | solution.py:19
  38.7 1.2 %collective-permute-start.6 = (bf16[1536,64]{0,1:T(8,128)(2,1)S(1)}, bf16[1536,64]{0,1:T(8,128)(2,1)S(1)}, u32[]{:S(2)}, u32[]{:S(2)}) collective-permute-start(bf16[1536,64]{0,1:T(8,128)(2,1)S(1)} %collective-permute-done.4), channel_id=1, source_target_pairs={{0,2},{2,4},{4,6},{6,8},{8,10},{10,12},{12,14},{14,0},{1,3},{3,5},... | collective-permute-start | bytes 589832 | tf_op jit(solution)/shard_map/ppermute | solution.py:19
  39.9 0.0 collective-permute-done.5
  40.0 8.8 %collective-permute-done.6 = bf16[1536,64]{0,1:T(8,128)(2,1)S(1)} collective-permute-done((bf16[1536,64]{0,1:T(8,128)(2,1)S(1)}, bf16[1536,64]{0,1:T(8,128)(2,1)S(1)}, u32[]{:S(2)}, u32[]{:S(2)}) %collective-permute-start.6) | collective-permute-done | bytes 196640 | tf_op jit(solution)/shard_map/ppermute | solution.py:19
  48.8 2.1 %gather_fusion = bf16[512,1536]{1,0:T(8,128)(2,1)S(1)} fusion(bf16[1536,512]{0,1:T(8,128)(2,1)S(1)} %constant_dynamic-update-slice_fusion, s32[1024]{0:T(1024)S(1)} %pad_clamp_fusion), kind=kCustom, calls=%fused_computation | custom fusion | bytes 3147776 | tf_op jit(solution)/shard_map/jit(_take)/gather | solution.py:28
  50.9 1.4 %fusion.6 = bf16[1536,512]{0,1:T(8,128)(2,1)} fusion(bf16[512,1536]{1,0:T(8,128)(2,1)S(1)} %gather_fusion, pred[512]{0:T(512)(128)(4,1)S(1)} %compare_and_fusion), kind=kLoop, calls=%fused_computation.6 | loop fusion | flops 786432 | bytes 3146240 | tf_op jit(solution)/shard_map/jit(_take)/select_n | solution.py:28
  52.3 0.0 all-gather.2.cloned.1.call-update
  52.3 0.0 reduce-scatter.2.cloned.1.call-start
  52.4 10.9 %all-gather.2.cloned.1.call-done = bf16[3072,512]{0,1:T(8,128)(2,1)} async-done(((bf16[1536,512]{0,1:T(8,128)(2,1)}), bf16[3072,512]{0,1:T(8,128)(2,1)}) %all-gather.2.cloned.1.call-update) | async-done | bytes 3145744 | tf_op jit(solution)/shard_map/all_gather | solution.py:31
  63.3 11.5 %fusion.5 = f32[512,512]{1,0:T(8,128)} fusion(bf16[512,1536]{1,0:T(8,128)(2,1)S(1)} %gather_fusion, pred[512]{0:T(512)(128)(4,1)S(1)} %compare_and_fusion, bf16[3072,512]{0,1:T(8,128)(2,1)} %all-gather.2.cloned.1.call-done, bf16[1,1536,3072]{2,1,0:T(8,128)(2,1)} %param.5), kind=kOutput, calls=%fused_computation.5 | convolution fusion | flops 5638717440 | bytes 15204864 | tf_op jit(solution)/shard_map/dot_general | solution.py:35
  74.8 0.0 copy-start.2
  74.8 0.0 copy-start.3
  74.8 0.0 reduce-scatter.2.cloned.1.call-update
  74.9 9.7 %reduce-scatter.2.cloned.1.call-done = f32[512,256]{1,0:T(8,128)} async-done(((f32[512,512]{1,0:T(8,128)}), f32[512,256]{1,0:T(8,128)}) %reduce-scatter.2.cloned.1.call-update) | async-done | bytes 524304 | tf_op jit(solution)/shard_map/reduce_scatter | solution.py:43
  84.6 2.4 %copy.13 = f32[1,512,256]{2,0,1:T(1,128)} copy(f32[1,512,256]{2,1,0:T(8,128)} %bitcast.16) | data formatting | bytes 1048576 | tf_op jit(solution)/shard_map/broadcast_in_dim | solution.py:47
  86.9 5.8 %all-to-all-start = ((f32[1,512,256]{2,0,1:T(1,128)}), f32[1,512,256]{2,0,1:T(1,128)S(1)}, u32[]{:S(2)}, u32[]{:S(2)}) async-start(f32[1,512,256]{2,0,1:T(1,128)} %copy.13), calls=%async_computation.1 | async-start | bytes 1048576 | tf_op jit(solution)/shard_map/all_to_all | solution.py:47
  92.7 0.0 copy-done.2
  92.7 0.0 copy-done.3
  92.7 0.2 select_reduce_fusion
  92.9 14.8 %all-to-all-done = f32[1,512,256]{2,0,1:T(1,128)S(1)} async-done(((f32[1,512,256]{2,0,1:T(1,128)}), f32[1,512,256]{2,0,1:T(1,128)S(1)}, u32[]{:S(2)}, u32[]{:S(2)}) %all-to-all-start) | async-done | bytes 524320 | tf_op jit(solution)/shard_map/all_to_all | solution.py:47
  107.7 0.8 fusion.9
  108.5 0.8 copy.15
  (11 shorter events, 0.2 us)
Async XLA Ops:
  6.5 6.9 %copy-start = (bf16[1536,64]{0,1:T(8,128)(2,1)S(1)}, bf16[1536,64]{0,1:T(8,128)(2,1)}, u32[]{:S(2)}) copy-start(bf16[1536,64]{0,1:T(8,128)(2,1)} %param.6) | copy-start | bytes 589828
  6.5 7.0 %copy-start.1 = (s32[512]{0:T(512)S(1)}, s32[512]{0:T(512)}, u32[]{:S(2)}) copy-start(s32[512]{0:T(512)} %param.7) | copy-start | bytes 6148
  6.5 56.8 %all-gather.2.cloned.1.call-start = ((), (), s32[]{:S(2)}) async-start(), calls=%async_computation.2 | async-start | bytes 4718592 | tf_op jit(solution)/shard_map/all_gather | solution.py:31
  6.5 11.7 %collective-permute-start = (bf16[1536,64]{0,1:T(8,128)(2,1)}, bf16[1536,64]{0,1:T(8,128)(2,1)S(1)}, u32[]{:S(2)}, u32[]{:S(2)}) collective-permute-start(bf16[1536,64]{0,1:T(8,128)(2,1)} %param.6), channel_id=1, source_target_pairs={{0,2},{2,4},{4,6},{6,8},{8,10},{10,12},{12,14},{14,0},{1,3},{3,5},... | collective-permute-start | bytes 589832 | tf_op jit(solution)/shard_map/ppermute | solution.py:19
  9.5 11.1 %collective-permute-start.1 = (bf16[1536,64]{0,1:T(8,128)(2,1)}, bf16[1536,64]{0,1:T(8,128)(2,1)S(1)}, u32[]{:S(2)}, u32[]{:S(2)}) collective-permute-start(bf16[1536,64]{0,1:T(8,128)(2,1)} %param.6), channel_id=1, source_target_pairs={{0,14},{2,0},{4,2},{6,4},{8,6},{10,8},{12,10},{14,12},{1,15},{3,1}... | collective-permute-start | bytes 589832 | tf_op jit(solution)/shard_map/ppermute | solution.py:24
  18.2 9.9 %collective-permute-start.2 = (bf16[1536,64]{0,1:T(8,128)(2,1)S(1)}, bf16[1536,64]{0,1:T(8,128)(2,1)S(1)}, u32[]{:S(2)}, u32[]{:S(2)}) collective-permute-start(bf16[1536,64]{0,1:T(8,128)(2,1)S(1)} %collective-permute-done), channel_id=1, source_target_pairs={{0,2},{2,4},{4,6},{6,8},{8,10},{10,12},{12,14},{14,0},{1,3},{3,5},... | collective-permute-start | bytes 589832 | tf_op jit(solution)/shard_map/ppermute | solution.py:19
  20.6 10.0 %collective-permute-start.3 = (bf16[1536,64]{0,1:T(8,128)(2,1)S(1)}, bf16[1536,64]{0,1:T(8,128)(2,1)S(1)}, u32[]{:S(2)}, u32[]{:S(2)}) collective-permute-start(bf16[1536,64]{0,1:T(8,128)(2,1)S(1)} %collective-permute-done.1), channel_id=1, source_target_pairs={{0,14},{2,0},{4,2},{6,4},{8,6},{10,8},{12,10},{14,12},{1,15},{3,1}... | collective-permute-start | bytes 589832 | tf_op jit(solution)/shard_map/ppermute | solution.py:24
  28.1 10.6 %collective-permute-start.4 = (bf16[1536,64]{0,1:T(8,128)(2,1)S(1)}, bf16[1536,64]{0,1:T(8,128)(2,1)S(1)}, u32[]{:S(2)}, u32[]{:S(2)}) collective-permute-start(bf16[1536,64]{0,1:T(8,128)(2,1)S(1)} %collective-permute-done.2), channel_id=1, source_target_pairs={{0,2},{2,4},{4,6},{6,8},{8,10},{10,12},{12,14},{14,0},{1,3},{3,5},... | collective-permute-start | bytes 589832 | tf_op jit(solution)/shard_map/ppermute | solution.py:19
  30.6 9.3 %collective-permute-start.5 = (bf16[1536,64]{0,1:T(8,128)(2,1)S(1)}, bf16[1536,64]{0,1:T(8,128)(2,1)S(1)}, u32[]{:S(2)}, u32[]{:S(2)}) collective-permute-start(bf16[1536,64]{0,1:T(8,128)(2,1)S(1)} %collective-permute-done.3), channel_id=1, source_target_pairs={{0,14},{2,0},{4,2},{6,4},{8,6},{10,8},{12,10},{14,12},{1,15},{3,1}... | collective-permute-start | bytes 589832 | tf_op jit(solution)/shard_map/ppermute | solution.py:24
  38.7 10.0 %collective-permute-start.6 = (bf16[1536,64]{0,1:T(8,128)(2,1)S(1)}, bf16[1536,64]{0,1:T(8,128)(2,1)S(1)}, u32[]{:S(2)}, u32[]{:S(2)}) collective-permute-start(bf16[1536,64]{0,1:T(8,128)(2,1)S(1)} %collective-permute-done.4), channel_id=1, source_target_pairs={{0,2},{2,4},{4,6},{6,8},{8,10},{10,12},{12,14},{14,0},{1,3},{3,5},... | collective-permute-start | bytes 589832 | tf_op jit(solution)/shard_map/ppermute | solution.py:19
  52.3 32.2 %reduce-scatter.2.cloned.1.call-start = ((), (), s32[]{:S(2)}) async-start(), calls=%async_computation.3 | async-start | bytes 1572864 | tf_op jit(solution)/shard_map/reduce_scatter | solution.py:43
  74.8 17.9 %copy-start.2 = (s32[4,8]{1,0:T(4,128)S(1)}, s32[4,8]{1,0:T(4,128)}, u32[]{:S(2)}) copy-start(s32[4,8]{1,0:T(4,128)} %param.8) | copy-start | bytes 388
  74.8 17.9 %copy-start.3 = (f32[64]{0:T(128)S(1)}, f32[64]{0:T(128)}, u32[]{:S(2)}) copy-start(f32[64]{0:T(128)} %param.9) | copy-start | bytes 772
  86.9 20.8 %all-to-all-start = ((f32[1,512,256]{2,0,1:T(1,128)}), f32[1,512,256]{2,0,1:T(1,128)S(1)}, u32[]{:S(2)}, u32[]{:S(2)}) async-start(f32[1,512,256]{2,0,1:T(1,128)} %copy.13), calls=%async_computation.1 | async-start | bytes 1048576 | tf_op jit(solution)/shard_map/all_to_all | solution.py:47
Sparse Core Ops, SparseCore 0:
  52.5 10.8 all-gather.1
  75.0 9.5 reduce-scatter.1
